TPU v7x, 32 devices: a whole 2x2x4 slice. The times are simulated.
32 devices in a mesh: grp: 4 (over y, x), dev: 8 (over z, core).
Axes of the slice: x: 2, y: 2, z: 4, core: 2. Of those that a mesh axis runs over, the one named last changes fastest.
Arguments:
- table: float32 [262144, 128], P(('grp', 'dev')), may hold values from -6 to 6
- cold_grads: float32 [131072, 128], P(('grp', 'dev')), may hold values from -6 to 6
- cold_owner: int32 [131072, 1], P(('grp', 'dev')), may hold values from 0 to 31; in each aligned block of 4096 rows (0 to 4095, 4096 to 8191, ...) at most 256 rows name the same one
- cold_row: int32 [131072], P(('grp', 'dev')), may hold values from 0 to 8191
- hot_grads: float32 [32768, 128], P(('grp', 'dev')), may hold values from -6 to 6
- hot_slot: int32 [32768], P(('grp', 'dev')), may hold values from 0 to 255
- hot_ids: int32 [256], replicated, may hold values from 0 to 262143, as said below
Outputs:
- new_table: float32 [262144, 128], P(('grp', 'dev'))
Inputs may be any that keep to these rules, and one draw needn't show every extreme that they name: `cold_owner`: among the 4096 rare-row lookups of one device no owner is named more than 256 times, a bound that some block reaches. `hot_ids`: all entries differ.
All inputs are finite; a program needn't handle non-finite values.
Results may differ from a plain program's by a relative error of at most 0.00005.
Values sent between devices are 32-bit elements; how exact they have to be, the bound alone decides.
A program may use at most 64 MiB of HBM per device.

v0:
```python
import functools

import jax
import jax.numpy as jnp
from jax import lax
from jax.experimental import pallas as pl
from jax.experimental.pallas import tpu as pltpu
from jax.sharding import PartitionSpec as P

LEARN = 0.05
MESH = pl.DeviceIdType.MESH
LANES = 128
CHUNK = 256
MIB = 1024 * 1024
TILE = 4096


def parts_of(values):
    high = values.astype(jnp.bfloat16)
    rest = values - high.astype(jnp.float32)
    middle = rest.astype(jnp.bfloat16)
    low = (rest - middle.astype(jnp.float32)).astype(jnp.bfloat16)
    return high, middle, low


def plan_kernel(slots, owner_ref, hot_grads_ref, hot_slot_ref, place_ref, count_ref, partial_ref):
    blocks = owner_ref.shape[0] * LANES // CHUNK
    lines = CHUNK // LANES
    tall = count_ref.shape[0]
    before = lax.broadcasted_iota(jnp.int32, (CHUNK, CHUNK), 0)
    after = lax.broadcasted_iota(jnp.int32, (CHUNK, CHUNK), 1)
    tri = (before <= after).astype(jnp.bfloat16)
    owners = lax.broadcasted_iota(jnp.int32, (tall, CHUNK), 0)
    base = owners.astype(jnp.float32)[:, 0:1] * slots - 1.0
    start = base
    for b in range(blocks):
        own = jnp.concatenate([owner_ref[b * lines + j:b * lines + j + 1, :] for j in range(lines)], axis=1)
        hit = own == owners
        run = jnp.dot(hit.astype(jnp.bfloat16), tri, preferred_element_type=jnp.float32) + base
        base = run[:, CHUNK - 1:CHUNK]
        spot = jnp.sum(jnp.where(hit, run, 0.0), axis=0, keepdims=True)
        whole = (spot + 0.5).astype(jnp.int32)
        for j in range(lines):
            r = b * lines + j
            place_ref[r:r + 1, :] = whole[:, j * LANES:(j + 1) * LANES]
    count_ref[...] = jnp.broadcast_to((base - start + 0.5).astype(jnp.int32), count_ref.shape)
    hot, width = partial_ref.shape
    looks = hot_grads_ref.shape[0]
    pick = lax.broadcasted_iota(jnp.int32, (hot, looks), 0) == hot_slot_ref[...]
    split = jnp.concatenate(parts_of(hot_grads_ref[...]), axis=1)
    three = jnp.dot(pick.astype(jnp.bfloat16), split, preferred_element_type=jnp.float32)
    partial_ref[...] = three[:, :width] + three[:, width:2 * width] + three[:, 2 * width:]


def pack_kernel(place_ref, row_ref, grads_ref, send_ref, rows_ref):
    step = 16

    def body(t, carry):
        first = pl.multiple_of(t * step, step)
        for j in range(step):
            to = place_ref[first + j]
            rows_ref[to] = row_ref[first + j]
            send_ref[pl.ds(to, 1), :] = grads_ref[pl.ds(first + j, 1), :]
        return carry

    lax.fori_loop(0, grads_ref.shape[0] // step, body, 0)


def partner(at, step, size):
    if size & (size - 1):
        return lax.rem(at + step, size), lax.rem(at - step + size, size)
    mixed = 0
    bit = 1
    while bit < size:
        mixed = mixed + bit * lax.rem(at // bit + step // bit, 2)
        bit *= 2
    return mixed, mixed


def exchange_kernel(
    n_grp, n_dev, slots, send_ref, meta_ref, part_ref, ids_ref, table_ref, acc,
    got, gmeta, total, rbuf, halves, s_big, r_big, s_meta, r_meta, s_rs, r_rs, s_ag, r_ag, s_own,
):
    devices = n_grp * n_dev
    width = acc.shape[1]
    rows_dev = acc.shape[0]
    tile = min(TILE, rows_dev)
    my_grp, my_dev = lax.axis_index("grp"), lax.axis_index("dev")
    me = my_grp * n_dev + my_dev
    barrier = pltpu.get_barrier_semaphore()

    def each(fn, first=1, last=devices):
        def body(k, carry):
            g, d = partner(my_grp, lax.rem(k, n_grp), n_grp)[0], partner(my_dev, k // n_grp, n_dev)[0]
            fn(k, g * n_dev + d, (g, d))
            return carry
        lax.fori_loop(first, last, body, 0)

    def remote(src, dst, ssem, rsem, where):
        return pltpu.make_async_remote_copy(
            src_ref=src, dst_ref=dst, send_sem=ssem, recv_sem=rsem,
            device_id=where, device_id_type=MESH,
        )

    load = pltpu.make_async_copy(table_ref, acc, s_own.at[0])
    load.start()
    own_big = pltpu.make_async_copy(send_ref.at[me], got.at[me], s_own.at[1])
    own_big.start()
    each(lambda k, p, w: pl.semaphore_signal(barrier, inc=1, device_id=w, device_id_type=MESH))
    pl.semaphore_wait(barrier, devices - 1)

    def big(k, p, w):
        remote(send_ref.at[p], got.at[me], s_big, r_big.at[k], w).start()

    most_sent = devices - devices // 4
    each(lambda k, p, w: remote(part_ref.at[p], rbuf.at[me], s_rs, r_rs, w).start())
    each(lambda k, p, w: remote(meta_ref.at[p], gmeta.at[me], s_meta, r_meta, w).start())
    each(big, 1, most_sent)
    rbuf[me] = part_ref[me]
    gmeta[me] = meta_ref[me]

    here = (my_grp, my_dev)
    most = pl.ds(0, devices - 1)

    def all_of(src, dst, ssem, rsem):
        return remote(src.at[most], dst.at[most], ssem, rsem, here)

    rs = all_of(part_ref, rbuf, s_rs, r_rs)
    rs.wait_recv()
    total[me] = jnp.sum(rbuf[...], axis=0)
    rs.wait_send()
    each(lambda k, p, w: remote(total.at[me], total.at[me], s_ag, r_ag, w).start())
    each(big, most_sent, devices)

    def add(values, ids):
        count = values.shape[0]
        high = values.astype(jnp.bfloat16)
        halves[0:count, 0:width] = high
        halves[0:count, width:2 * width] = (values - high.astype(jnp.float32)).astype(jnp.bfloat16)
        spot = lax.broadcasted_iota(jnp.int32, (tile, count), 0)

        def body(t, carry):
            at = pl.multiple_of(t * tile, tile)
            hit = jnp.where(spot == ids - at, 1.0, 0.0).astype(jnp.bfloat16)
            both = jnp.dot(hit, halves[0:count, :], preferred_element_type=jnp.float32)
            w = pl.ds(at, tile)
            acc[w, :] = acc[w, :] - LEARN * (both[:, :width] + both[:, width:])
            return carry

        lax.fori_loop(0, rows_dev // tile, body, 0)

    lines = -(-slots // LANES)

    def add_block(source):
        info = gmeta[source]
        filled = info[lines:lines + 1, :]
        ids = jnp.concatenate([info[j:j + 1, :] for j in range(lines)], axis=1)[:, :slots]
        held = jnp.concatenate([filled] * lines, axis=1)[:, :slots]
        ids = jnp.where(lax.broadcasted_iota(jnp.int32, (1, slots), 1) < held, ids, -1)
        block = got[source]
        deep = lax.broadcasted_iota(jnp.int32, block.shape, 0)
        add(jnp.where(deep < filled[:, :width], block, 0.0), ids)

    load.wait()
    own_big.wait()
    add_block(me)
    metas = all_of(meta_ref, gmeta, s_meta, r_meta)
    metas.wait_send()
    metas.wait_recv()

    def arrived(k, carry):
        g, d = partner(my_grp, lax.rem(k, n_grp), n_grp)[1], partner(my_dev, k // n_grp, n_dev)[1]
        source = g * n_dev + d
        remote(send_ref.at[0], got.at[source], s_big, r_big.at[k], here).wait_recv()
        add_block(source)
        return carry

    lax.fori_loop(1, most_sent, arrived, 0)
    ag = all_of(total, total, s_ag, r_ag)
    ag.wait_send()
    ag.wait_recv()
    hot = ids_ref.shape[1]
    add(total[...].reshape(-1, width)[:hot], ids_ref[...] - me * rows_dev)
    lax.fori_loop(most_sent, devices, arrived, 0)
    remote(send_ref.at[most], got.at[most], s_big, r_big.at[0], here).wait_send()


def on_device(n_grp, n_dev, table, cold_grads, cold_owner, cold_row, hot_grads, hot_slot, hot_ids):
    devices = n_grp * n_dev
    width = table.shape[1]
    lookups = cold_grads.shape[0]
    rows_dev = table.shape[0]
    hot = hot_ids.shape[0]
    slots = max(4, 2 * lookups // devices)
    tall = -(-devices // 8) * 8
    vmem, smem, hbm = (pl.BlockSpec(memory_space=m) for m in (pltpu.VMEM, pltpu.SMEM, pl.ANY))
    f32, i32 = jnp.float32, jnp.int32
    place, count, partial = pl.pallas_call(
        functools.partial(plan_kernel, slots),
        out_shape=(
            jax.ShapeDtypeStruct((lookups // LANES, LANES), i32),
            jax.ShapeDtypeStruct((tall, LANES), i32),
            jax.ShapeDtypeStruct((hot, width), f32),
        ),
        in_specs=[vmem] * 3,
        out_specs=(vmem,) * 3,
        compiler_params=pltpu.CompilerParams(vmem_limit_bytes=8 * MIB),
        cost_estimate=pl.CostEstimate(flops=0, bytes_accessed=4 * MIB, transcendentals=0),
        name="plan",
    )(cold_owner.reshape(-1, LANES), hot_grads, hot_slot.reshape(1, -1))
    send, rows = pl.pallas_call(
        pack_kernel,
        out_shape=(
            jax.ShapeDtypeStruct((devices * slots, width), f32),
            jax.ShapeDtypeStruct((devices * slots,), i32),
        ),
        in_specs=[smem, smem, vmem],
        out_specs=(vmem, smem),
        compiler_params=pltpu.CompilerParams(vmem_limit_bytes=12 * MIB),
        cost_estimate=pl.CostEstimate(flops=0, bytes_accessed=24 * MIB, transcendentals=0),
        name="pack",
    )(place.reshape(-1), cold_row, cold_grads)
    lines = -(-slots // LANES)
    rows = jnp.pad(rows.reshape(devices, slots), ((0, 0), (0, lines * LANES - slots)))
    height = 4 if lines < 4 else -(-(lines + 1) // 8) * 8
    meta = jnp.concatenate(
        [rows.reshape(devices, lines, LANES),
         jnp.broadcast_to(count[:devices, None, :], (devices, height - lines, LANES))], axis=1,
    )
    share = -(-hot // devices)
    partial = jnp.pad(partial, ((0, share * devices - hot), (0, 0))).reshape(devices, share, width)
    dma = pltpu.SemaphoreType.DMA
    return pl.pallas_call(
        functools.partial(exchange_kernel, n_grp, n_dev, slots),
        out_shape=jax.ShapeDtypeStruct(table.shape, f32),
        in_specs=[hbm, vmem, vmem, vmem, hbm],
        out_specs=vmem,
        scratch_shapes=[
            pltpu.VMEM((devices, slots, width), f32),
            pltpu.VMEM(meta.shape, i32),
            pltpu.VMEM(partial.shape, f32),
            pltpu.VMEM(partial.shape, f32),
            pltpu.VMEM((max(slots, hot), 2 * width), jnp.bfloat16),
            dma, dma((devices,)), dma, dma, dma, dma, dma, dma, dma((2,)),
        ],
        compiler_params=pltpu.CompilerParams(
            collective_id=0, has_side_effects=True, vmem_limit_bytes=32 * MIB
        ),
        name="exchange",
    )(send.reshape(devices, slots, width), meta, partial,
      hot_ids.reshape(1, -1), table)


def solution(mesh):
    in_specs = (
        P(("grp", "dev"), None),
        P(("grp", "dev"), None),
        P(("grp", "dev"), None),
        P(("grp", "dev")),
        P(("grp", "dev"), None),
        P(("grp", "dev")),
        P(),
    )
    out_specs = P(("grp", "dev"), None)
    return jax.shard_map(
        functools.partial(on_device, mesh.shape["grp"], mesh.shape["dev"]),
        mesh=mesh, in_specs=in_specs, out_specs=out_specs, check_vma=False,
    )
```

profile of v0, /device:TPU:17, one launch (start us, length us, event | category | flops | bytes accessed | tf_op | source)
XLA Modules:
  0.0 127.3 jit_solution(677802145214254581)
XLA Ops:
  0.0 0.0 copy-start.2
  0.0 1.0 copy-done.2
  1.0 0.0 copy-start.4
  1.0 0.7 copy-done.4
  1.8 0.0 copy-start.5
  1.8 0.7 copy-done.5
  2.4 1.3 plan.1
  3.7 0.0 copy-start.1
  3.7 1.6 %copy-done.1 = f32[4096,128]{1,0:T(8,128)S(1)} copy-done((f32[4096,128]{1,0:T(8,128)S(1)}, f32[4096,128]{1,0:T(8,128)}, u32[]{:S(2)}) %copy-start.1) | copy-done | bytes 2097176
  5.3 0.0 copy-start.3
  5.3 0.7 copy-done.3
  6.0 9.6 %pack.1 = (f32[8192,128]{1,0:T(8,128)S(1)}, s32[8192]{0:T(1024)S(1)}) custom-call(s32[4096]{0:T(1024)S(1)} %bitcast.10, s32[4096]{0:T(1024)S(1)} %copy-done.3, f32[4096,128]{1,0:T(8,128)S(1)} %copy-done.1), custom_call_target="tpu_custom_call" | custom-call | bytes 25165824 | tf_op jit(solution)/shard_map/pack/pallas_call | solution.py:211
  15.7 0.0 copy-start
  15.7 2.2 %copy-done = f32[8192,128]{1,0:T(8,128)S(1)} copy-done((f32[8192,128]{1,0:T(8,128)S(1)}, f32[8192,128]{1,0:T(8,128)}, u32[]{:S(2)}) %copy-start) | copy-done | bytes 4194328
  17.9 0.0 copy-start.6
  17.9 0.7 copy-done.6
  18.6 106.7 %exchange.1 = f32[8192,128]{1,0:T(8,128)S(1)} custom-call(f32[32,256,128]{2,1,0:T(8,128)S(1)} %bitcast.7, s32[32,4,128]{2,1,0:T(4,128)S(1)} %pad_add_fusion.meta_ref, f32[32,8,128]{2,1,0:T(8,128)S(1)} %bitcast.8, s32[1,256]{1,0:T(1,128)S(1)} %bitcast.13, f32[8192,128]{1,0:T(8,128)S(1)} %copy-done), custom_call_target="tpu_custom_call" | custom-call | tf_op jit(solution)/shard_map/exchange/pallas_call | solution.py:233
  125.3 2.0 %copy.9 = f32[8192,128]{1,0:T(8,128)} copy(f32[8192,128]{1,0:T(8,128)S(1)} %exchange.1) | data formatting | bytes 8388608
  (2 shorter events, 0.0 us)
Async XLA Ops:
  0.0 1.0 copy-start.2
  1.0 0.7 copy-start.4
  1.8 0.7 copy-start.5
  3.7 1.6 %copy-start.1 = (f32[4096,128]{1,0:T(8,128)S(1)}, f32[4096,128]{1,0:T(8,128)}, u32[]{:S(2)}) copy-start(f32[4096,128]{1,0:T(8,128)} %grads_ref.1) | copy-start | bytes 6291460
  5.3 0.7 copy-start.3
  15.7 2.2 %copy-start = (f32[8192,128]{1,0:T(8,128)S(1)}, f32[8192,128]{1,0:T(8,128)}, u32[]{:S(2)}) copy-start(f32[8192,128]{1,0:T(8,128)} %table_ref.1) | copy-start | bytes 12582916
  17.9 0.7 copy-start.6
where the time goes:
time: 129 us; the launch traced here: 127 us
  Pallas kernels  118 us (91%)
  local copies, waits for them, and re-layouts  9.64 us (7%)
    pallas_call x1, Pallas kernels, on_device(): pl.pallas_call(functools.partial(exchange_kernel, n_grp, n_dev, slots), o...  107 us
    unnamed x15, local copies, waits for them, and re-layouts  9.62 us
    pallas_call x1, Pallas kernels, on_device(): pl.pallas_call(pack_kernel, out_shape=(jax.ShapeDtypeStruct((devices * sl...  9.6 us

commit v1 on v0

v1 whole, which is shorter than its diff:
```python
import functools

import jax
import jax.numpy as jnp
from jax import lax
from jax.experimental import pallas as pl
from jax.experimental.pallas import tpu as pltpu
from jax.sharding import PartitionSpec as P

LEARN = 0.05
MESH = pl.DeviceIdType.MESH
LANES = 128
CHUNK = 256
MIB = 1024 * 1024
TILE = 4096
STEP = 16
AHEAD = 8


def parts_of(values):
    high = values.astype(jnp.bfloat16)
    rest = values - high.astype(jnp.float32)
    middle = rest.astype(jnp.bfloat16)
    low = (rest - middle.astype(jnp.float32)).astype(jnp.bfloat16)
    return high, middle, low


def partner(at, step, size):
    if size & (size - 1):
        return lax.rem(at + step, size), lax.rem(at - step + size, size)
    mixed = 0
    bit = 1
    while bit < size:
        mixed = mixed + bit * lax.rem(at // bit + step // bit, 2)
        bit *= 2
    return mixed, mixed


def spread(i, size):
    if size & (size - 1):
        return i
    turned = 0
    bit = 1
    while bit < size:
        turned = turned + (size // (2 * bit)) * lax.rem(i // bit, 2)
        bit *= 2
    return turned


def plan_kernel(slots, owner_hbm, row_hbm, place, meta, owner, row, spots, s_in):
    devices, lines = meta.shape[0], meta.shape[1]
    deep = lines * LANES
    tall = place.shape[0]
    loads = [pltpu.make_async_copy(owner_hbm, owner, s_in.at[0]), pltpu.make_async_copy(row_hbm, row, s_in.at[1])]
    for load in loads:
        load.start()
    for load in loads:
        load.wait()
    before = lax.broadcasted_iota(jnp.int32, (CHUNK, CHUNK), 0)
    after = lax.broadcasted_iota(jnp.int32, (CHUNK, CHUNK), 1)
    tri = (before <= after).astype(jnp.bfloat16)
    owners = lax.broadcasted_iota(jnp.int32, (tall, CHUNK), 0)
    lane = lax.broadcasted_iota(jnp.int32, (tall, CHUNK), 1).astype(jnp.float32)
    slot = lax.broadcasted_iota(jnp.int32, (deep, CHUNK), 0)
    base = jnp.full((tall, 1), -1.0, jnp.float32)
    found = jnp.zeros((4 * tall, deep), jnp.float32)
    per = CHUNK // LANES
    for b in range(owner.shape[0] // per):
        own = jnp.concatenate([owner[b * per + j:b * per + j + 1, :] for j in range(per)], axis=1)
        at = jnp.concatenate([row[b * per + j:b * per + j + 1, :] for j in range(per)], axis=1)
        hit = own == owners
        run = jnp.dot(hit.astype(jnp.bfloat16), tri, preferred_element_type=jnp.float32) + base
        base = run[:, CHUNK - 1:CHUNK]
        spot = jnp.sum(jnp.where(hit, run, 0.0), axis=0, keepdims=True)
        taken = (slot == (spot + 0.5).astype(jnp.int32)).astype(jnp.bfloat16)
        high = (at // LANES + 1).astype(jnp.float32)
        low = lax.rem(at, LANES).astype(jnp.float32)
        fields = jnp.concatenate([
            jnp.where(hit, float(b), 0.0), jnp.where(hit, lane, 0.0),
            jnp.where(hit, high, 0.0), jnp.where(hit, low, 0.0),
        ], axis=0).astype(jnp.bfloat16)
        found = found + lax.dot_general(
            fields, taken, (((1,), (1,)), ((), ())), preferred_element_type=jnp.float32)
    whole = (found + 0.5).astype(jnp.int32)
    place[...] = whole[:tall] * CHUNK + whole[tall:2 * tall]
    rows = (whole[2 * tall:3 * tall] - 1) * LANES + whole[3 * tall:]
    for j in range(lines):
        spots[j] = rows[:, j * LANES:(j + 1) * LANES]

    def lay_meta(p, carry):
        for j in range(lines):
            meta[p, j:j + 1, :] = spots[j, pl.ds(p, 1), :]
        return carry

    lax.fori_loop(0, devices, lay_meta, 0)


def kernel(
    n_grp, n_dev, slots, place, meta, grads, hot_grads, hot_slot, hot_ids, table_hbm, acc,
    gmeta, send, got, halves, part, rbuf, zbuf, total, s_in, s_meta, r_meta, s_big, r_big, s_hot, r_hot,
):
    devices = n_grp * n_dev
    rows_dev, width = acc.shape
    tile = min(TILE, rows_dev)
    lines = meta.shape[1]
    n_lo = 2 if n_dev % 2 == 0 else 1
    n_hi = n_dev // n_lo
    plane = n_grp * n_lo
    my_grp, my_dev = lax.axis_index("grp"), lax.axis_index("dev")
    my_hi, my_lo = my_dev // n_lo, lax.rem(my_dev, n_lo)
    me = my_grp * n_dev + my_dev
    seat = my_grp * n_lo + my_lo
    here = (my_grp, my_dev)
    barrier = pltpu.get_barrier_semaphore()

    load = pltpu.make_async_copy(table_hbm, acc, s_in)
    load.start()

    def at_step(k, side):
        a = n_grp - 1 - k // n_dev
        b = spread(n_dev - 1 - lax.rem(k, n_dev), n_dev)
        g, d = partner(my_grp, a, n_grp)[side], partner(my_dev, b, n_dev)[side]
        return g * n_dev + d, (g, d)

    def remote(src, dst, ssem, rsem, where):
        return pltpu.make_async_remote_copy(
            src_ref=src, dst_ref=dst, send_sem=ssem, recv_sem=rsem,
            device_id=where, device_id_type=MESH,
        )

    def repeat(first, last, fn):
        def body(k, carry):
            fn(k)
            return carry
        lax.fori_loop(first, last, body, 0)

    repeat(0, devices - 1, lambda k: pl.semaphore_signal(
        barrier, inc=1, device_id=at_step(k, 0)[1], device_id_type=MESH))

    def gather(p, out):
        def body(t, carry):
            first = pl.multiple_of(t * STEP, STEP)
            for j in range(STEP):
                out[p, pl.ds(first + j, 1), :] = grads[pl.ds(place[p, first + j], 1), :]
            return carry
        lax.fori_loop(0, slots // STEP, body, 0)

    def pack(k):
        gather(at_step(k, 0)[0], send)

    def launch(k):
        p, where = at_step(k, 0)
        remote(send.at[p], got.at[me], s_big, r_big.at[k], where).start()

    ahead = min(AHEAD, devices - 1)
    repeat(0, ahead // 2, pack)
    pl.semaphore_wait(barrier, devices - 1)
    repeat(0, ahead // 2, launch)

    def send_meta(k):
        p, where = at_step(k, 0)
        remote(meta.at[p], gmeta.at[me], s_meta, r_meta, where).start()

    repeat(0, devices - 1, send_meta)
    gmeta[me] = meta[me]

    def across(buf_from, at_from, buf_to, at_to, sems):
        def one(j):
            g, lo = partner(my_grp, j // n_lo, n_grp)[0], partner(my_lo, lax.rem(j, n_lo), n_lo)[0]
            src = at_from(g * n_lo + lo)
            remote(buf_from.at[src], buf_to.at[at_to], s_hot.at[sems], r_hot.at[sems], (g, my_hi * n_lo + lo)).start()
        repeat(1, plane, one)

    def finish(buf, count, sems):
        if count:
            most = pl.ds(0, count)
            done = remote(buf.at[most], buf.at[most], s_hot.at[sems], r_hot.at[sems], here)
            done.wait_recv()
            done.wait_send()

    hot = plane * part.shape[1]
    pick = lax.broadcasted_iota(jnp.int32, (hot, hot_grads.shape[0]), 0) == hot_slot[...]
    split = jnp.concatenate(parts_of(hot_grads[...]), axis=1)
    three = jnp.dot(pick.astype(jnp.bfloat16), split, preferred_element_type=jnp.float32)
    part[...] = (three[:, :width] + three[:, width:2 * width] + three[:, 2 * width:]).reshape(part.shape)
    repeat(ahead // 2, ahead, pack)
    repeat(ahead // 2, ahead - 1, launch)
    across(part, lambda other: other, rbuf, seat, 0)
    rbuf[seat] = part[seat]
    gather(me, got)
    load.wait()
    finish(rbuf, plane - 1, 0)
    zbuf[my_hi] = jnp.sum(rbuf[...], axis=0)

    def up(j):
        hi = partner(my_hi, j, n_hi)[0]
        remote(zbuf.at[my_hi], zbuf.at[my_hi], s_hot.at[1], r_hot.at[1], (my_grp, hi * n_lo + my_lo)).start()

    metas = remote(meta.at[pl.ds(0, devices - 1)], gmeta.at[pl.ds(0, devices - 1)], s_meta, r_meta, here)

    def add(values, ids):
        count = values.shape[0]
        high = values.astype(jnp.bfloat16)
        halves[0:count, 0:width] = high
        halves[0:count, width:2 * width] = (values - high.astype(jnp.float32)).astype(jnp.bfloat16)
        spot = lax.broadcasted_iota(jnp.int32, (tile, count), 0)

        def body(t, carry):
            at = pl.multiple_of(t * tile, tile)
            hit = jnp.where(spot == ids - at, 1.0, 0.0).astype(jnp.bfloat16)
            both = jnp.dot(hit, halves[0:count, :], preferred_element_type=jnp.float32)
            w = pl.ds(at, tile)
            acc[w, :] = acc[w, :] - LEARN * (both[:, :width] + both[:, width:])
            return carry

        lax.fori_loop(0, rows_dev // tile, body, 0)

    def turn(i):
        k = lax.rem(i + devices - 1, devices)

        @pl.when(i + ahead < devices - 1)
        def _():
            pack(i + ahead)

        @pl.when(i + ahead < devices)
        def _():
            launch(i + ahead - 1)

        @pl.when(i == 0)
        def _():
            repeat(1, n_hi, up)

        @pl.when(i == 1)
        def _():
            metas.wait_send()
            metas.wait_recv()

        @pl.when(i == devices // 4)
        def _():
            finish(zbuf, n_hi - 1, 1)
            total[seat] = jnp.sum(zbuf[...], axis=0)

        @pl.when(i == devices // 4 + 1)
        def _():
            across(total, lambda other: seat, total, seat, 2)

        @pl.when(i == devices * 5 // 8)
        def _():
            finish(total, plane - 1, 2)
            count = hot_ids.shape[1]
            add(total[...].reshape(-1, width)[:count], hot_ids[...] - me * rows_dev)

        source = at_step(k, 1)[0]

        @pl.when(i > 0)
        def _():
            remote(send.at[0], got.at[source], s_big, r_big.at[k], here).wait_recv()

        info = gmeta[source]
        ids = jnp.concatenate([info[j:j + 1, :] for j in range(lines)], axis=1)[:, :slots]
        add(got[source], ids)

    repeat(0, devices, turn)
    most = pl.ds(0, devices - 1)
    remote(send.at[most], got.at[most], s_big, r_big.at[0], here).wait_send()


def on_device(n_grp, n_dev, table, cold_grads, cold_owner, cold_row, hot_grads, hot_slot, hot_ids):
    devices = n_grp * n_dev
    rows_dev, width = table.shape
    lookups = cold_grads.shape[0]
    looks = hot_grads.shape[0]
    hot = hot_ids.shape[0]
    slots = -(-2 * lookups // devices // STEP) * STEP
    tall = -(-devices // 8) * 8
    lines = -(-slots // LANES)
    n_lo = 2 if n_dev % 2 == 0 else 1
    plane = n_grp * n_lo
    share = -(-hot // (plane * 8)) * 8
    vmem, hbm = pl.BlockSpec(memory_space=pltpu.VMEM), pl.BlockSpec(memory_space=pltpu.HBM)
    f32, i32 = jnp.float32, jnp.int32
    dma = pltpu.SemaphoreType.DMA
    smem = pl.BlockSpec(memory_space=pltpu.SMEM)
    place, meta = pl.pallas_call(
        functools.partial(plan_kernel, slots),
        out_shape=(
            jax.ShapeDtypeStruct((tall, lines * LANES), i32),
            jax.ShapeDtypeStruct((devices, lines, LANES), i32),
        ),
        in_specs=[hbm] * 2,
        out_specs=(vmem,) * 2,
        scratch_shapes=[
            pltpu.VMEM((lookups // LANES, LANES), i32),
            pltpu.VMEM((lookups // LANES, LANES), i32),
            pltpu.VMEM((lines, tall, LANES), i32),
            dma((2,)),
        ],
        compiler_params=pltpu.CompilerParams(vmem_limit_bytes=8 * MIB),
        cost_estimate=pl.CostEstimate(flops=10 ** 9, bytes_accessed=MIB, transcendentals=0),
        name="plan",
    )(cold_owner.reshape(-1, LANES), cold_row.reshape(-1, LANES))
    blocks = (devices, slots, width)
    shares = (plane, share, width)
    return pl.pallas_call(
        functools.partial(kernel, n_grp, n_dev, slots),
        out_shape=jax.ShapeDtypeStruct(table.shape, f32),
        in_specs=[smem, vmem, vmem, vmem, vmem, vmem, hbm],
        out_specs=vmem,
        scratch_shapes=[
            pltpu.VMEM((devices, lines, LANES), i32),
            pltpu.VMEM(blocks, f32),
            pltpu.VMEM(blocks, f32),
            pltpu.VMEM((max(slots, hot), 2 * width), jnp.bfloat16),
            pltpu.VMEM(shares, f32),
            pltpu.VMEM(shares, f32),
            pltpu.VMEM((n_dev // n_lo, share, width), f32),
            pltpu.VMEM(shares, f32),
            dma, dma, dma, dma, dma((devices,)), dma((3,)), dma((3,)),
        ],
        compiler_params=pltpu.CompilerParams(
            collective_id=0, has_side_effects=True, vmem_limit_bytes=44 * MIB
        ),
        name="update",
    )(place, meta, cold_grads, hot_grads, hot_slot.reshape(1, -1), hot_ids.reshape(1, -1), table)


def solution(mesh):
    in_specs = (
        P(("grp", "dev"), None),
        P(("grp", "dev"), None),
        P(("grp", "dev"), None),
        P(("grp", "dev")),
        P(("grp", "dev"), None),
        P(("grp", "dev")),
        P(),
    )
    out_specs = P(("grp", "dev"), None)
    return jax.shard_map(
        functools.partial(on_device, mesh.shape["grp"], mesh.shape["dev"]),
        mesh=mesh, in_specs=in_specs, out_specs=out_specs, check_vma=False,
    )
```

time: 129 us -> 121 us (0.938)
  Pallas kernels: 118 us -> 114 us
  local copies, waits for them, and re-layouts: 9.64 us -> 6 us
    pallas_call x2 -> x1, Pallas kernels: 116 us -> 112 us  [on_device(): pl.pallas_call(functools.partial(kernel, n_grp, n_dev, slots), out_shape=...]
    unnamed x15 -> x13, local copies, waits for them, and re-layouts: 9.62 us -> 6 us
where the time goes in v1:
time: 121 us; the launch traced here: 120 us
  Pallas kernels  114 us (94%)
  local copies, waits for them, and re-layouts  6 us (5%)
    pallas_call x1, Pallas kernels, on_device(): pl.pallas_call(functools.partial(kernel, n_grp, n_dev, slots), out_shape=...  112 us
    unnamed x13, local copies, waits for them, and re-layouts  6 us

profile of v1, /device:TPU:17, one launch (start us, length us, event | category | flops | bytes accessed | tf_op | source)
XLA Modules:
  0.0 120.0 jit_solution(10736576709469134225)
XLA Ops:
  0.0 0.0 copy-start
  0.0 0.0 copy-start.4
  0.0 0.9 copy-done.4
  0.9 0.0 copy-start.5
  0.9 0.7 copy-done.5
  1.6 2.3 %plan.1 = (s32[32,256]{1,0:T(8,128)S(1)}, s32[32,2,128]{2,1,0:T(2,128)S(1)}) custom-call(s32[32,128]{1,0:T(8,128)S(1)} %bitcast.6, s32[32,128]{1,0:T(8,128)S(1)} %bitcast.7), custom_call_target="tpu_custom_call" | custom-call | flops 1000000000 | bytes 1048576 | tf_op jit(solution)/shard_map/plan/pallas_call | solution.py:284
  3.9 0.0 copy-done
  3.9 0.0 copy-start.1
  3.9 1.0 copy-done.1
  4.9 0.0 copy-start.2
  4.9 0.7 copy-done.2
  5.6 0.0 copy-start.3
  5.6 0.7 copy-done.3
  6.3 111.7 %update.1 = f32[8192,128]{1,0:T(8,128)S(1)} custom-call(s32[32,256]{1,0:T(8,128)S(1)} %get-tuple-element.7.place, s32[32,2,128]{2,1,0:T(2,128)S(1)} %get-tuple-element.8.meta, f32[4096,128]{1,0:T(8,128)S(1)} %copy-done, f32[1024,128]{1,0:T(8,128)S(1)} %copy-done.1, s32[1,1024]{1,0:T(1,128)S(1)} %bitcast.4, s32[1,256]{1,0:T(1,128)S(1)} %bitcast.5, ...), custom_call_target="tpu_custom_call" | custom-call | tf_op jit(solution)/shard_map/update/pallas_call | solution.py:304
  118.0 2.0 %copy.9 = f32[8192,128]{1,0:T(8,128)} copy(f32[8192,128]{1,0:T(8,128)S(1)} %update.1) | data formatting | bytes 8388608
Async XLA Ops:
  0.0 3.9 %copy-start = (f32[4096,128]{1,0:T(8,128)S(1)}, f32[4096,128]{1,0:T(8,128)}, u32[]{:S(2)}) copy-start(f32[4096,128]{1,0:T(8,128)} %grads.1) | copy-start | bytes 6291460
  0.0 0.9 copy-start.4
  0.9 0.7 copy-start.5
  3.9 1.0 copy-start.1
  4.9 0.7 copy-start.2
  5.6 0.7 copy-start.3

commit v2 on v1

--- a/solution.py
+++ b/solution.py
@@ -14,7 +14,8 @@
 MIB = 1024 * 1024
 TILE = 4096
 STEP = 16
-AHEAD = 8
+FINISH = 2048
+FIRST, SECOND, THIRD, LAST = 4, 8, 14, 24
 
 
 def parts_of(values):
@@ -23,6 +24,17 @@
     middle = rest.astype(jnp.bfloat16)
     low = (rest - middle.astype(jnp.float32)).astype(jnp.bfloat16)
     return high, middle, low
+
+
+def ids_of(info, slots):
+    return jnp.concatenate([info[j:j + 1, :] for j in range(info.shape[0])], axis=1)[:, :slots]
+
+
+def split_into(halves, values):
+    count, width = values.shape
+    high = values.astype(jnp.bfloat16)
+    halves[0:count, 0:width] = high
+    halves[0:count, width:2 * width] = (values - high.astype(jnp.float32)).astype(jnp.bfloat16)
 
 
 def partner(at, step, size):
@@ -47,15 +59,10 @@
     return turned
 
 
-def plan_kernel(slots, owner_hbm, row_hbm, place, meta, owner, row, spots, s_in):
+def plan_kernel(slots, rows_dev, code_ref, place, meta, spots):
     devices, lines = meta.shape[0], meta.shape[1]
     deep = lines * LANES
     tall = place.shape[0]
-    loads = [pltpu.make_async_copy(owner_hbm, owner, s_in.at[0]), pltpu.make_async_copy(row_hbm, row, s_in.at[1])]
-    for load in loads:
-        load.start()
-    for load in loads:
-        load.wait()
     before = lax.broadcasted_iota(jnp.int32, (CHUNK, CHUNK), 0)
     after = lax.broadcasted_iota(jnp.int32, (CHUNK, CHUNK), 1)
     tri = (before <= after).astype(jnp.bfloat16)
@@ -65,9 +72,9 @@
     base = jnp.full((tall, 1), -1.0, jnp.float32)
     found = jnp.zeros((4 * tall, deep), jnp.float32)
     per = CHUNK // LANES
-    for b in range(owner.shape[0] // per):
-        own = jnp.concatenate([owner[b * per + j:b * per + j + 1, :] for j in range(per)], axis=1)
-        at = jnp.concatenate([row[b * per + j:b * per + j + 1, :] for j in range(per)], axis=1)
+    for b in range(code_ref.shape[0] // per):
+        code = jnp.concatenate([code_ref[b * per + j:b * per + j + 1, :] for j in range(per)], axis=1)
+        own, at = code // rows_dev, lax.rem(code, rows_dev)
         hit = own == owners
         run = jnp.dot(hit.astype(jnp.bfloat16), tri, preferred_element_type=jnp.float32) + base
         base = run[:, CHUNK - 1:CHUNK]
@@ -96,7 +103,7 @@
 
 
 def kernel(
-    n_grp, n_dev, slots, place, meta, grads, hot_grads, hot_slot, hot_ids, table_hbm, acc,
+    n_grp, n_dev, slots, place, meta, grads, hot_grads, hot_slot, hot_ids, table_hbm, acc, block, info,
     gmeta, send, got, halves, part, rbuf, zbuf, total, s_in, s_meta, r_meta, s_big, r_big, s_hot, r_hot,
 ):
     devices = n_grp * n_dev
@@ -116,9 +123,13 @@
     load = pltpu.make_async_copy(table_hbm, acc, s_in)
     load.start()
 
+    half = n_dev // 2
+    own = half * n_grp
+
     def at_step(k, side):
-        a = n_grp - 1 - k // n_dev
-        b = spread(n_dev - 1 - lax.rem(k, n_dev), n_dev)
+        a = lax.rem(k, n_grp)
+        b = k // n_grp
+        b = jnp.where(a == 0, lax.rem(b + n_dev - half, n_dev), b)
         g, d = partner(my_grp, a, n_grp)[side], partner(my_dev, b, n_dev)[side]
         return g * n_dev + d, (g, d)
 
@@ -134,7 +145,14 @@
             return carry
         lax.fori_loop(first, last, body, 0)
 
-    repeat(0, devices - 1, lambda k: pl.semaphore_signal(
+    def others(first, last, fn):
+        def one(k):
+            @pl.when(k != own)
+            def _():
+                fn(k)
+        repeat(first, last, one)
+
+    others(0, devices, lambda k: pl.semaphore_signal(
         barrier, inc=1, device_id=at_step(k, 0)[1], device_id_type=MESH))
 
     def gather(p, out):
@@ -152,17 +170,16 @@
         p, where = at_step(k, 0)
         remote(send.at[p], got.at[me], s_big, r_big.at[k], where).start()
 
-    ahead = min(AHEAD, devices - 1)
-    repeat(0, ahead // 2, pack)
-    pl.semaphore_wait(barrier, devices - 1)
-    repeat(0, ahead // 2, launch)
+    def pack_then_launch(k):
+        pack(k)
+
+        @pl.when(k - 1 != own)
+        def _():
+            launch(k - 1)
 
     def send_meta(k):
         p, where = at_step(k, 0)
         remote(meta.at[p], gmeta.at[me], s_meta, r_meta, where).start()
-
-    repeat(0, devices - 1, send_meta)
-    gmeta[me] = meta[me]
 
     def across(buf_from, at_from, buf_to, at_to, sems):
         def one(j):
@@ -178,31 +195,46 @@
             done.wait_recv()
             done.wait_send()
 
+    def up(j):
+        hi = partner(my_hi, j, n_hi)[0]
+        remote(zbuf.at[my_hi], zbuf.at[my_hi], s_hot.at[1], r_hot.at[1], (my_grp, hi * n_lo + my_lo)).start()
+
+    pack(0)
+    pack(1)
+    pl.semaphore_wait(barrier, devices - 1)
+    launch(0)
+    repeat(2, FIRST, pack_then_launch)
+    others(0, devices, send_meta)
     hot = plane * part.shape[1]
     pick = lax.broadcasted_iota(jnp.int32, (hot, hot_grads.shape[0]), 0) == hot_slot[...]
     split = jnp.concatenate(parts_of(hot_grads[...]), axis=1)
     three = jnp.dot(pick.astype(jnp.bfloat16), split, preferred_element_type=jnp.float32)
     part[...] = (three[:, :width] + three[:, width:2 * width] + three[:, 2 * width:]).reshape(part.shape)
-    repeat(ahead // 2, ahead, pack)
-    repeat(ahead // 2, ahead - 1, launch)
+    gmeta[me] = meta[me]
+    rbuf[seat] = part[seat]
+    cuts = [FIRST, FIRST + 1, SECOND, SECOND + 1, THIRD, THIRD + 1, devices]
+    repeat(cuts[0], cuts[1], pack_then_launch)
     across(part, lambda other: other, rbuf, seat, 0)
-    rbuf[seat] = part[seat]
-    gather(me, got)
-    load.wait()
+    repeat(cuts[1], cuts[2], pack_then_launch)
     finish(rbuf, plane - 1, 0)
     zbuf[my_hi] = jnp.sum(rbuf[...], axis=0)
-
-    def up(j):
-        hi = partner(my_hi, j, n_hi)[0]
-        remote(zbuf.at[my_hi], zbuf.at[my_hi], s_hot.at[1], r_hot.at[1], (my_grp, hi * n_lo + my_lo)).start()
+    repeat(cuts[2], cuts[3], pack_then_launch)
+    repeat(1, n_hi, up)
+    repeat(cuts[3], cuts[4], pack_then_launch)
+    finish(zbuf, n_hi - 1, 1)
+    total[seat] = jnp.sum(zbuf[...], axis=0)
+    repeat(cuts[4], cuts[5], pack_then_launch)
+    across(total, lambda other: seat, total, seat, 2)
+    repeat(cuts[5], cuts[6], pack_then_launch)
+    gather(me, got)
+    others(devices - 1, devices, launch)
+    load.wait()
 
     metas = remote(meta.at[pl.ds(0, devices - 1)], gmeta.at[pl.ds(0, devices - 1)], s_meta, r_meta, here)
 
     def add(values, ids):
         count = values.shape[0]
-        high = values.astype(jnp.bfloat16)
-        halves[0:count, 0:width] = high
-        halves[0:count, width:2 * width] = (values - high.astype(jnp.float32)).astype(jnp.bfloat16)
+        split_into(halves, values)
         spot = lax.broadcasted_iota(jnp.int32, (tile, count), 0)
 
         def body(t, carry):
@@ -215,36 +247,11 @@
 
         lax.fori_loop(0, rows_dev // tile, body, 0)
 
-    def turn(i):
-        k = lax.rem(i + devices - 1, devices)
-
-        @pl.when(i + ahead < devices - 1)
-        def _():
-            pack(i + ahead)
-
-        @pl.when(i + ahead < devices)
-        def _():
-            launch(i + ahead - 1)
-
-        @pl.when(i == 0)
-        def _():
-            repeat(1, n_hi, up)
-
-        @pl.when(i == 1)
-        def _():
-            metas.wait_send()
-            metas.wait_recv()
-
-        @pl.when(i == devices // 4)
-        def _():
-            finish(zbuf, n_hi - 1, 1)
-            total[seat] = jnp.sum(zbuf[...], axis=0)
-
-        @pl.when(i == devices // 4 + 1)
-        def _():
-            across(total, lambda other: seat, total, seat, 2)
-
-        @pl.when(i == devices * 5 // 8)
+    metas.wait_send()
+    metas.wait_recv()
+
+    def turn(k):
+        @pl.when(k == LAST)
         def _():
             finish(total, plane - 1, 2)
             count = hot_ids.shape[1]
@@ -252,17 +259,40 @@
 
         source = at_step(k, 1)[0]
 
-        @pl.when(i > 0)
+        @pl.when(k != own)
         def _():
             remote(send.at[0], got.at[source], s_big, r_big.at[k], here).wait_recv()
 
-        info = gmeta[source]
-        ids = jnp.concatenate([info[j:j + 1, :] for j in range(lines)], axis=1)[:, :slots]
-        add(got[source], ids)
+        @pl.when(k < devices - 1)
+        def _():
+            add(got[source], ids_of(gmeta[source], slots))
+
+        @pl.when(k == devices - 1)
+        def _():
+            block[...] = got[source]
+            info[...] = gmeta[source]
 
     repeat(0, devices, turn)
     most = pl.ds(0, devices - 1)
     remote(send.at[most], got.at[most], s_big, r_big.at[0], here).wait_send()
+
+
+def finish_kernel(slots, acc, block, info, out, ready, halves, sems):
+    rows_dev, width = acc.shape
+    tile = min(FINISH, rows_dev)
+    ids = ids_of(info[...], slots)
+    split_into(halves, block[...])
+    spot = lax.broadcasted_iota(jnp.int32, (tile, slots), 0)
+    copies = []
+    for t in range(rows_dev // tile):
+        w = pl.ds(t * tile, tile)
+        hit = jnp.where(spot == ids - t * tile, 1.0, 0.0).astype(jnp.bfloat16)
+        both = jnp.dot(hit, halves[...], preferred_element_type=jnp.float32)
+        ready[w, :] = acc[w, :] - LEARN * (both[:, :width] + both[:, width:])
+        copies.append(pltpu.make_async_copy(ready.at[w], out.at[w], sems.at[t]))
+        copies[-1].start()
+    for copy in copies:
+        copy.wait()
 
 
 def on_device(n_grp, n_dev, table, cold_grads, cold_owner, cold_row, hot_grads, hot_slot, hot_ids):
@@ -282,30 +312,29 @@
     dma = pltpu.SemaphoreType.DMA
     smem = pl.BlockSpec(memory_space=pltpu.SMEM)
     place, meta = pl.pallas_call(
-        functools.partial(plan_kernel, slots),
+        functools.partial(plan_kernel, slots, rows_dev),
         out_shape=(
             jax.ShapeDtypeStruct((tall, lines * LANES), i32),
             jax.ShapeDtypeStruct((devices, lines, LANES), i32),
         ),
-        in_specs=[hbm] * 2,
+        in_specs=[vmem],
         out_specs=(vmem,) * 2,
-        scratch_shapes=[
-            pltpu.VMEM((lookups // LANES, LANES), i32),
-            pltpu.VMEM((lookups // LANES, LANES), i32),
-            pltpu.VMEM((lines, tall, LANES), i32),
-            dma((2,)),
-        ],
+        scratch_shapes=[pltpu.VMEM((lines, tall, LANES), i32)],
         compiler_params=pltpu.CompilerParams(vmem_limit_bytes=8 * MIB),
-        cost_estimate=pl.CostEstimate(flops=10 ** 9, bytes_accessed=MIB, transcendentals=0),
+        cost_estimate=pl.CostEstimate(flops=10 ** 11, bytes_accessed=MIB, transcendentals=0),
         name="plan",
-    )(cold_owner.reshape(-1, LANES), cold_row.reshape(-1, LANES))
+    )(cold_owner.reshape(-1, LANES) * rows_dev + cold_row.reshape(-1, LANES))
     blocks = (devices, slots, width)
     shares = (plane, share, width)
-    return pl.pallas_call(
+    acc, block, info = pl.pallas_call(
         functools.partial(kernel, n_grp, n_dev, slots),
-        out_shape=jax.ShapeDtypeStruct(table.shape, f32),
+        out_shape=(
+            jax.ShapeDtypeStruct(table.shape, f32),
+            jax.ShapeDtypeStruct(blocks[1:], f32),
+            jax.ShapeDtypeStruct((lines, LANES), i32),
+        ),
         in_specs=[smem, vmem, vmem, vmem, vmem, vmem, hbm],
-        out_specs=vmem,
+        out_specs=(vmem,) * 3,
         scratch_shapes=[
             pltpu.VMEM((devices, lines, LANES), i32),
             pltpu.VMEM(blocks, f32),
@@ -322,6 +351,19 @@
         ),
         name="update",
     )(place, meta, cold_grads, hot_grads, hot_slot.reshape(1, -1), hot_ids.reshape(1, -1), table)
+    return pl.pallas_call(
+        functools.partial(finish_kernel, slots),
+        out_shape=jax.ShapeDtypeStruct(table.shape, f32),
+        in_specs=[vmem] * 3,
+        out_specs=hbm,
+        scratch_shapes=[
+            pltpu.VMEM(table.shape, f32),
+            pltpu.VMEM((slots, 2 * width), jnp.bfloat16),
+            dma((-(-rows_dev // FINISH),)),
+        ],
+        compiler_params=pltpu.CompilerParams(vmem_limit_bytes=24 * MIB),
+        name="finish",
+    )(acc, block, info)
 
 
 def solution(mesh):

time: 121 us -> 109 us (0.901)
  Pallas kernels: 114 us -> 107 us
  local copies, waits for them, and re-layouts: 6 us -> 0.02 us
  other arithmetic: 0 us -> 1.46 us
    pallas_call x1, Pallas kernels: 112 us -> 102 us  [on_device(): pl.pallas_call(functools.partial(kernel, n_grp, n_dev, slots), out_shape=...]
    unnamed x13 -> x8, local copies, waits for them, and re-layouts: 6 us -> 0.02 us
    pallas_call x1 -> x2, Pallas kernels: 2.28 us -> 5.09 us  [the longest x1 2.86 us: on_device(): pl.pallas_call(functools.partial(finish_kernel, slots), out_shape=jax.Sha...]
where the time goes in v2:
time: 109 us; the launch traced here: 108 us
  Pallas kernels  107 us (98%)
  other arithmetic  1.46 us (1%)
    pallas_call x1, Pallas kernels, on_device(): pl.pallas_call(functools.partial(kernel, n_grp, n_dev, slots), out_shape=...  102 us
    pallas_call x1, Pallas kernels, on_device(): pl.pallas_call(functools.partial(finish_kernel, slots), out_shape=jax.Sha...  2.86 us
    pallas_call x1, Pallas kernels, on_device(): pl.pallas_call(functools.partial(plan_kernel, slots, rows_dev), out_shape...  2.24 us

profile of v2, /device:TPU:17, one launch (start us, length us, event | category | flops | bytes accessed | tf_op | source)
XLA Modules:
  0.0 108.4 jit_solution(16777377659745084760)
XLA Ops:
  0.0 0.7 broadcast_multiply_fusion
  0.7 0.7 bitcast_add_fusion.code_ref
  1.5 0.0 copy-start
  1.5 0.0 copy-start.1
  1.5 0.0 copy-start.2
  1.5 0.0 copy-start.3
  1.5 2.2 %plan.1 = (s32[32,256]{1,0:T(8,128)S(1)}, s32[32,2,128]{2,1,0:T(2,128)S(1)}) custom-call(s32[32,128]{1,0:T(8,128)S(1)} %bitcast_add_fusion.code_ref), custom_call_target="tpu_custom_call" | custom-call | flops 99999997952 | bytes 1048576 | tf_op jit(solution)/shard_map/plan/pallas_call | solution.py:314
  3.7 0.0 copy-done
  3.7 0.0 copy-done.1
  3.7 0.0 copy-done.2
  3.8 0.0 copy-done.3
  3.8 101.8 %update.1 = (f32[8192,128]{1,0:T(8,128)S(1)}, f32[256,128]{1,0:T(8,128)S(1)}, s32[2,128]{1,0:T(2,128)S(1)}) custom-call(s32[32,256]{1,0:T(8,128)S(1)} %get-tuple-element.10.place, s32[32,2,128]{2,1,0:T(2,128)S(1)} %get-tuple-element.11.meta, f32[4096,128]{1,0:T(8,128)S(1)} %copy-done, f32[1024,128]{1,0:T(8,128)S(1)} %copy-done.1, s32[1,1024]{1,0:T(1,128)S(1)} %bitcast.5, ...), custom_call_target="tpu_custom_call" | custom-call | tf_op jit(solution)/shard_map/update/pallas_call | solution.py:329
  105.5 2.9 %finish.1 = f32[8192,128]{1,0:T(8,128)} custom-call(f32[8192,128]{1,0:T(8,128)S(1)} %get-tuple-element.12.acc, f32[256,128]{1,0:T(8,128)S(1)} %get-tuple-element.13.block, s32[2,128]{1,0:T(2,128)S(1)} %get-tuple-element.14.info), custom_call_target="tpu_custom_call" | custom-call | tf_op jit(solution)/shard_map/finish/pallas_call | solution.py:354
Async XLA Ops:
  1.5 2.3 %copy-start = (f32[4096,128]{1,0:T(8,128)S(1)}, f32[4096,128]{1,0:T(8,128)}, u32[]{:S(2)}) copy-start(f32[4096,128]{1,0:T(8,128)} %grads.1) | copy-start | bytes 6291460
  1.5 2.3 %copy-start.1 = (f32[1024,128]{1,0:T(8,128)S(1)}, f32[1024,128]{1,0:T(8,128)}, u32[]{:S(2)}) copy-start(f32[1024,128]{1,0:T(8,128)} %hot_grads.1) | copy-start | bytes 1572868
  1.5 2.3 %copy-start.2 = (s32[1024]{0:T(1024)S(1)}, s32[1024]{0:T(1024)}, u32[]{:S(2)}) copy-start(s32[1024]{0:T(1024)} %param.12) | copy-start | bytes 12292
  1.5 2.3 %copy-start.3 = (s32[256]{0:T(256)S(1)}, s32[256]{0:T(256)}, u32[]{:S(2)}) copy-start(s32[256]{0:T(256)} %param.13) | copy-start | bytes 3076

commit v3 on v2

--- a/solution.py
+++ b/solution.py
@@ -110,7 +110,7 @@
     rows_dev, width = acc.shape
     tile = min(TILE, rows_dev)
     lines = meta.shape[1]
-    n_lo = 2 if n_dev % 2 == 0 else 1
+    n_lo = n_dev // 2 if n_dev % 2 == 0 else 1
     n_hi = n_dev // n_lo
     plane = n_grp * n_lo
     my_grp, my_dev = lax.axis_index("grp"), lax.axis_index("dev")
@@ -152,8 +152,12 @@
                 fn(k)
         repeat(first, last, one)
 
-    others(0, devices, lambda k: pl.semaphore_signal(
-        barrier, inc=1, device_id=at_step(k, 0)[1], device_id_type=MESH))
+    for g in range(n_grp):
+        def greet(d, g=g):
+            @pl.when(g * n_dev + d != me)
+            def _():
+                pl.semaphore_signal(barrier, inc=1, device_id=(g, d), device_id_type=MESH)
+        repeat(0, n_dev, greet)
 
     def gather(p, out):
         def body(t, carry):
@@ -304,7 +308,7 @@
     slots = -(-2 * lookups // devices // STEP) * STEP
     tall = -(-devices // 8) * 8
     lines = -(-slots // LANES)
-    n_lo = 2 if n_dev % 2 == 0 else 1
+    n_lo = n_dev // 2 if n_dev % 2 == 0 else 1
     plane = n_grp * n_lo
     share = -(-hot // (plane * 8)) * 8
     vmem, hbm = pl.BlockSpec(memory_space=pltpu.VMEM), pl.BlockSpec(memory_space=pltpu.HBM)
@@ -323,7 +327,7 @@
         compiler_params=pltpu.CompilerParams(vmem_limit_bytes=8 * MIB),
         cost_estimate=pl.CostEstimate(flops=10 ** 11, bytes_accessed=MIB, transcendentals=0),
         name="plan",
-    )(cold_owner.reshape(-1, LANES) * rows_dev + cold_row.reshape(-1, LANES))
+    )((cold_owner * rows_dev + cold_row.reshape(-1, 1)).reshape(-1, LANES))
     blocks = (devices, slots, width)
     shares = (plane, share, width)
     acc, block, info = pl.pallas_call(

time: 109 us -> 106 us (0.972)
  Pallas kernels: 107 us -> 105 us
    pallas_call x1, Pallas kernels: 102 us -> 100 us  [on_device(): pl.pallas_call(functools.partial(kernel, n_grp, n_dev, slots), out_shape=...]
where the time goes in v3:
time: 106 us
  Pallas kernels  105 us (99%)
    pallas_call x1, Pallas kernels, on_device(): pl.pallas_call(functools.partial(kernel, n_grp, n_dev, slots), out_shape=...  100 us
    pallas_call x1, Pallas kernels, on_device(): pl.pallas_call(functools.partial(finish_kernel, slots), out_shape=jax.Sha...  2.86 us
    pallas_call x1, Pallas kernels, on_device(): pl.pallas_call(functools.partial(plan_kernel, slots, rows_dev), out_shape...  2.24 us

profile of v3, /device:TPU:17, one launch (start us, length us, event | category | flops | bytes accessed | tf_op | source)
XLA Modules:
  0.0 106.1 jit_solution(6832628750515264926)
XLA Ops:
  0.0 0.8 multiply_add_fusion
  0.8 0.0 copy-start
  0.8 0.0 copy-start.1
  0.8 0.0 copy-start.2
  0.8 0.0 copy-start.3
  0.8 2.2 %plan.1 = (s32[32,256]{1,0:T(8,128)S(1)}, s32[32,2,128]{2,1,0:T(2,128)S(1)}) custom-call(s32[32,128]{1,0:T(8,128)S(1)} %bitcast.4), custom_call_target="tpu_custom_call" | custom-call | flops 99999997952 | bytes 1048576 | tf_op jit(solution)/shard_map/plan/pallas_call | solution.py:318
  3.1 0.0 copy-done
  3.1 0.0 copy-done.1
  3.1 0.0 copy-done.2
  3.1 0.0 copy-done.3
  3.1 100.1 %update.1 = (f32[8192,128]{1,0:T(8,128)S(1)}, f32[256,128]{1,0:T(8,128)S(1)}, s32[2,128]{1,0:T(2,128)S(1)}) custom-call(s32[32,256]{1,0:T(8,128)S(1)} %get-tuple-element.10.place, s32[32,2,128]{2,1,0:T(2,128)S(1)} %get-tuple-element.11.meta, f32[4096,128]{1,0:T(8,128)S(1)} %copy-done, f32[1024,128]{1,0:T(8,128)S(1)} %copy-done.1, s32[1,1024]{1,0:T(1,128)S(1)} %bitcast.5, ...), custom_call_target="tpu_custom_call" | custom-call | tf_op jit(solution)/shard_map/update/pallas_call | solution.py:333
  103.2 2.9 %finish.1 = f32[8192,128]{1,0:T(8,128)} custom-call(f32[8192,128]{1,0:T(8,128)S(1)} %get-tuple-element.12.acc, f32[256,128]{1,0:T(8,128)S(1)} %get-tuple-element.13.block, s32[2,128]{1,0:T(2,128)S(1)} %get-tuple-element.14.info), custom_call_target="tpu_custom_call" | custom-call | tf_op jit(solution)/shard_map/finish/pallas_call | solution.py:358
Async XLA Ops:
  0.8 2.3 %copy-start = (f32[4096,128]{1,0:T(8,128)S(1)}, f32[4096,128]{1,0:T(8,128)}, u32[]{:S(2)}) copy-start(f32[4096,128]{1,0:T(8,128)} %grads.1) | copy-start | bytes 6291460
  0.8 2.3 %copy-start.1 = (f32[1024,128]{1,0:T(8,128)S(1)}, f32[1024,128]{1,0:T(8,128)}, u32[]{:S(2)}) copy-start(f32[1024,128]{1,0:T(8,128)} %hot_grads.1) | copy-start | bytes 1572868
  0.8 2.3 %copy-start.2 = (s32[1024]{0:T(1024)S(1)}, s32[1024]{0:T(1024)}, u32[]{:S(2)}) copy-start(s32[1024]{0:T(1024)} %param.12) | copy-start | bytes 12292
  0.8 2.3 %copy-start.3 = (s32[256]{0:T(256)S(1)}, s32[256]{0:T(256)}, u32[]{:S(2)}) copy-start(s32[256]{0:T(256)} %param.13) | copy-start | bytes 3076

commit v4 on v3

--- a/solution.py
+++ b/solution.py
@@ -14,7 +14,7 @@
 MIB = 1024 * 1024
 TILE = 4096
 STEP = 16
-FINISH = 2048
+FINISH = 1024
 FIRST, SECOND, THIRD, LAST = 4, 8, 14, 24
 
 
@@ -70,7 +70,7 @@
     lane = lax.broadcasted_iota(jnp.int32, (tall, CHUNK), 1).astype(jnp.float32)
     slot = lax.broadcasted_iota(jnp.int32, (deep, CHUNK), 0)
     base = jnp.full((tall, 1), -1.0, jnp.float32)
-    found = jnp.zeros((4 * tall, deep), jnp.float32)
+    left, right = [], []
     per = CHUNK // LANES
     for b in range(code_ref.shape[0] // per):
         code = jnp.concatenate([code_ref[b * per + j:b * per + j + 1, :] for j in range(per)], axis=1)
@@ -86,8 +86,11 @@
             jnp.where(hit, float(b), 0.0), jnp.where(hit, lane, 0.0),
             jnp.where(hit, high, 0.0), jnp.where(hit, low, 0.0),
         ], axis=0).astype(jnp.bfloat16)
-        found = found + lax.dot_general(
-            fields, taken, (((1,), (1,)), ((), ())), preferred_element_type=jnp.float32)
+        left.append(fields)
+        right.append(taken)
+    found = lax.dot_general(
+        jnp.concatenate(left, axis=1), jnp.concatenate(right, axis=1),
+        (((1,), (1,)), ((), ())), preferred_element_type=jnp.float32)
     whole = (found + 0.5).astype(jnp.int32)
     place[...] = whole[:tall] * CHUNK + whole[tall:2 * tall]
     rows = (whole[2 * tall:3 * tall] - 1) * LANES + whole[3 * tall:]
@@ -99,7 +102,7 @@
             meta[p, j:j + 1, :] = spots[j, pl.ds(p, 1), :]
         return carry
 
-    lax.fori_loop(0, devices, lay_meta, 0)
+    lax.fori_loop(0, devices, lay_meta, 0, unroll=8 if devices % 8 == 0 else 1)
 
 
 def kernel(

time: 106 us -> 106 us (level)
  no operation moved by 1% of the time
where the time goes in v4:
time: 106 us; the launch traced here: 105 us
  Pallas kernels  104 us (98%)
    pallas_call x1, Pallas kernels, on_device(): pl.pallas_call(functools.partial(kernel, n_grp, n_dev, slots), out_shape=...  100 us
    pallas_call x1, Pallas kernels, on_device(): pl.pallas_call(functools.partial(finish_kernel, slots), out_shape=jax.Sha...  2.62 us

profile of v4, /device:TPU:17, one launch (start us, length us, event | category | flops | bytes accessed | tf_op | source)
XLA Modules:
  0.0 105.2 jit_solution(14769347459610752606)
XLA Ops:
  0.0 0.8 multiply_add_fusion
  0.8 0.0 copy-start
  0.8 0.0 copy-start.1
  0.8 0.0 copy-start.2
  0.8 0.0 copy-start.3
  0.8 1.5 %plan.1 = (s32[32,256]{1,0:T(8,128)S(1)}, s32[32,2,128]{2,1,0:T(2,128)S(1)}) custom-call(s32[32,128]{1,0:T(8,128)S(1)} %bitcast.4), custom_call_target="tpu_custom_call" | custom-call | flops 99999997952 | bytes 1048576 | tf_op jit(solution)/shard_map/plan/pallas_call | solution.py:321
  2.3 0.0 copy-done
  2.4 0.1 copy-done.1
  2.4 0.0 copy-done.2
  2.4 0.0 copy-done.3
  2.4 100.1 %update.1 = (f32[8192,128]{1,0:T(8,128)S(1)}, f32[256,128]{1,0:T(8,128)S(1)}, s32[2,128]{1,0:T(2,128)S(1)}) custom-call(s32[32,256]{1,0:T(8,128)S(1)} %get-tuple-element.10.place, s32[32,2,128]{2,1,0:T(2,128)S(1)} %get-tuple-element.11.meta, f32[4096,128]{1,0:T(8,128)S(1)} %copy-done, f32[1024,128]{1,0:T(8,128)S(1)} %copy-done.1, s32[1,1024]{1,0:T(1,128)S(1)} %bitcast.5, ...), custom_call_target="tpu_custom_call" | custom-call | tf_op jit(solution)/shard_map/update/pallas_call | solution.py:336
  102.6 2.6 %finish.1 = f32[8192,128]{1,0:T(8,128)} custom-call(f32[8192,128]{1,0:T(8,128)S(1)} %get-tuple-element.12.acc, f32[256,128]{1,0:T(8,128)S(1)} %get-tuple-element.13.block, s32[2,128]{1,0:T(2,128)S(1)} %get-tuple-element.14.info), custom_call_target="tpu_custom_call" | custom-call | tf_op jit(solution)/shard_map/finish/pallas_call | solution.py:361
Async XLA Ops:
  0.8 1.6 %copy-start = (f32[4096,128]{1,0:T(8,128)S(1)}, f32[4096,128]{1,0:T(8,128)}, u32[]{:S(2)}) copy-start(f32[4096,128]{1,0:T(8,128)} %grads.1) | copy-start | bytes 6291460
  0.8 1.7 %copy-start.1 = (f32[1024,128]{1,0:T(8,128)S(1)}, f32[1024,128]{1,0:T(8,128)}, u32[]{:S(2)}) copy-start(f32[1024,128]{1,0:T(8,128)} %hot_grads.1) | copy-start | bytes 1572868
  0.8 1.7 %copy-start.2 = (s32[1024]{0:T(1024)S(1)}, s32[1024]{0:T(1024)}, u32[]{:S(2)}) copy-start(s32[1024]{0:T(1024)} %param.12) | copy-start | bytes 12292
  0.8 1.6 %copy-start.3 = (s32[256]{0:T(256)S(1)}, s32[256]{0:T(256)}, u32[]{:S(2)}) copy-start(s32[256]{0:T(256)} %param.13) | copy-start | bytes 3076

commit v5 on v4

--- a/solution.py
+++ b/solution.py
@@ -14,7 +14,7 @@
 MIB = 1024 * 1024
 TILE = 4096
 STEP = 16
-FINISH = 1024
+FINISH = 512
 FIRST, SECOND, THIRD, LAST = 4, 8, 14, 24
 
 

time: 106 us -> 105 us (level)
  no operation moved by 1% of the time
where the time goes in v5:
time: 105 us
  Pallas kernels  104 us (99%)
    pallas_call x1, Pallas kernels, on_device(): pl.pallas_call(functools.partial(kernel, n_grp, n_dev, slots), out_shape=...  100 us
    pallas_call x1, Pallas kernels, on_device(): pl.pallas_call(functools.partial(finish_kernel, slots), out_shape=jax.Sha...  2.55 us

profile of v5, /device:TPU:17, one launch (start us, length us, event | category | flops | bytes accessed | tf_op | source)
XLA Modules:
  0.0 105.1 jit_solution(3744475984785029453)
XLA Ops:
  0.0 0.8 multiply_add_fusion
  0.8 0.0 copy-start
  0.8 0.0 copy-start.1
  0.8 0.0 copy-start.2
  0.8 0.0 copy-start.3
  0.8 1.5 %plan.1 = (s32[32,256]{1,0:T(8,128)S(1)}, s32[32,2,128]{2,1,0:T(2,128)S(1)}) custom-call(s32[32,128]{1,0:T(8,128)S(1)} %bitcast.4), custom_call_target="tpu_custom_call" | custom-call | flops 99999997952 | bytes 1048576 | tf_op jit(solution)/shard_map/plan/pallas_call | solution.py:321
  2.3 0.0 copy-done
  2.4 0.1 copy-done.1
  2.4 0.0 copy-done.2
  2.4 0.0 copy-done.3
  2.4 100.1 %update.1 = (f32[8192,128]{1,0:T(8,128)S(1)}, f32[256,128]{1,0:T(8,128)S(1)}, s32[2,128]{1,0:T(2,128)S(1)}) custom-call(s32[32,256]{1,0:T(8,128)S(1)} %get-tuple-element.10.place, s32[32,2,128]{2,1,0:T(2,128)S(1)} %get-tuple-element.11.meta, f32[4096,128]{1,0:T(8,128)S(1)} %copy-done, f32[1024,128]{1,0:T(8,128)S(1)} %copy-done.1, s32[1,1024]{1,0:T(1,128)S(1)} %bitcast.5, ...), custom_call_target="tpu_custom_call" | custom-call | tf_op jit(solution)/shard_map/update/pallas_call | solution.py:336
  102.6 2.6 %finish.1 = f32[8192,128]{1,0:T(8,128)} custom-call(f32[8192,128]{1,0:T(8,128)S(1)} %get-tuple-element.12.acc, f32[256,128]{1,0:T(8,128)S(1)} %get-tuple-element.13.block, s32[2,128]{1,0:T(2,128)S(1)} %get-tuple-element.14.info), custom_call_target="tpu_custom_call" | custom-call | tf_op jit(solution)/shard_map/finish/pallas_call | solution.py:361
Async XLA Ops:
  0.8 1.6 %copy-start = (f32[4096,128]{1,0:T(8,128)S(1)}, f32[4096,128]{1,0:T(8,128)}, u32[]{:S(2)}) copy-start(f32[4096,128]{1,0:T(8,128)} %grads.1) | copy-start | bytes 6291460
  0.8 1.7 %copy-start.1 = (f32[1024,128]{1,0:T(8,128)S(1)}, f32[1024,128]{1,0:T(8,128)}, u32[]{:S(2)}) copy-start(f32[1024,128]{1,0:T(8,128)} %hot_grads.1) | copy-start | bytes 1572868
  0.8 1.7 %copy-start.2 = (s32[1024]{0:T(1024)S(1)}, s32[1024]{0:T(1024)}, u32[]{:S(2)}) copy-start(s32[1024]{0:T(1024)} %param.12) | copy-start | bytes 12292
  0.8 1.6 %copy-start.3 = (s32[256]{0:T(256)S(1)}, s32[256]{0:T(256)}, u32[]{:S(2)}) copy-start(s32[256]{0:T(256)} %param.13) | copy-start | bytes 3076
